TPU v7x, 128 devices: a whole 4x4x4 slice. The times are simulated.
128 devices in a mesh: depth: 16 (over z, y_hi, core), coef: 8 (over y_lo, x).
Axes of the slice: x: 4, y: 4 (y_hi: 2, y_lo: 2; y = y_hi * 2 + y_lo), z: 4, core: 2. Of those that a mesh axis runs over, the one named last changes fastest.
Arguments:
- volume: bfloat16 [64, 256, 64, 512], P('depth', None, 'coef'), may hold values from -1 to 1
- shift: int32 [64], P('depth'), may hold values from -64 to 64
- frac: int32 [64], P('depth'), may hold values from 0 to 16
- basis: bfloat16 [64, 64], replicated, may hold values from -0.75 to 0.75
- data: float32 [256, 64, 512], P(('depth', 'coef')), may hold values from 0.05 to 4
- mask: int32 [256, 64, 512], P(('depth', 'coef')), may hold values 0 or 1
Outputs:
- gradient: bfloat16 [64, 256, 64, 512], P('depth', None, 'coef')
- residual: bfloat16 [256, 64, 512], P(('depth', 'coef'))
All inputs are finite; a program needn't handle non-finite values. No bound on the sum of `mask` on one device may be relied on, other than what follows from the above.
Results may differ from a plain program's by a relative error of at most 0.0053.
Values may be sent and summed in bfloat16 or wider, within the bound.
A program may use at most 128 MiB of HBM per device.

v0:
```python
import jax
import jax.numpy as jnp
from jax import lax
from jax.sharding import PartitionSpec as P


def layer_tables(shift, frac, columns):
    position = jnp.arange(columns, dtype=jnp.int32)
    target = position[None, :, None] - shift[:, None, None]
    weight = frac.astype(jnp.float32)[:, None, None] / 16.0
    column = position[None, None, :]
    matrix = jnp.where(column == target, 1.0 - weight, 0.0) + jnp.where(
        column == target - 1, weight, 0.0
    )
    return matrix.astype(jnp.bfloat16)


def project_rows(volume_rows, interp):
    running = None
    for layer in range(volume_rows.shape[0]):
        slab = lax.dot_general(
            volume_rows[layer],
            interp[layer],
            (((2,), (1,)), ((), ())),
            preferred_element_type=jnp.float32,
        )
        running = slab if running is None else running + slab
    return running


def project_back(grad_rows, interp):
    slabs = []
    for layer in range(interp.shape[0]):
        slab = lax.dot_general(
            grad_rows, interp[layer], (((2,), (0,)), ((), ())), preferred_element_type=jnp.float32
        )
        slabs.append(slab.astype(jnp.bfloat16))
    return jnp.stack(slabs, axis=0)


def shards(volume, shift, frac, basis, data, mask):
    interp = layer_tables(shift, frac, volume.shape[3])
    coef_width = volume.shape[2]
    owned_rows = lax.psum_scatter(
        project_rows(volume, interp), "depth", scatter_dimension=0, tiled=True
    )
    complete = lax.all_to_all(owned_rows, "coef", split_axis=0, concat_axis=1, tiled=True)
    predicted = jnp.einsum(
        "ykx,kg->ygx", complete, basis.astype(jnp.float32), precision=lax.Precision.HIGHEST
    )
    residual = (mask.astype(jnp.float32) * (predicted - jnp.sqrt(data))).astype(jnp.bfloat16)
    start_k = lax.axis_index("coef") * coef_width
    local_basis = lax.dynamic_slice_in_dim(basis, start_k, coef_width, 0)
    grad_proj = (
        2.0
        * jnp.einsum(
            "ygx,kg->ykx",
            lax.all_gather(residual, ("depth", "coef"), axis=0, tiled=True),
            local_basis,
            preferred_element_type=jnp.float32,
        )
    ).astype(jnp.bfloat16)
    gradient = project_back(grad_proj, interp)
    return (gradient, residual)


def solution(mesh):
    in_specs = (
        P("depth", None, "coef", None),
        P("depth"),
        P("depth"),
        P(),
        P(("depth", "coef"), None, None),
        P(("depth", "coef"), None, None),
    )
    out_specs = (P("depth", None, "coef", None), P(("depth", "coef"), None, None))
    return jax.shard_map(shards, mesh=mesh, in_specs=in_specs, out_specs=out_specs, check_vma=False)
```

profile of v0, /device:TPU:1, one launch (start us, length us, event | category | flops | bytes accessed | tf_op | source)
XLA Modules:
  0.0 481.0 jit_solution(15174535884854855615)
XLA Ops:
  7.2 0.0 reduce-scatter.2.cloned.1.call-start
  7.2 0.7 broadcast_subtract_fusion
  7.9 0.7 iota_subtract_fusion
  8.6 3.8 fusion.17
  12.4 1.0 add_convert_fusion
  13.4 1.3 fusion
  14.8 1.3 fusion.1
  16.1 1.3 fusion.2
  17.4 3.6 add_bitcast_fusion
  21.0 5.6 %copy.35 = f32[256,8,512]{2,1,0:T(8,128)} copy(f32[256,8,512]{0,2,1:T(8,128)} %add_bitcast_fusion) | data formatting | bytes 8388608 | tf_op jit(solution)/shard_map/add | solution.py:27
  26.6 0.0 reduce-scatter.2.cloned.1.call-update
  26.6 0.0 all-gather.2.cloned.1.call-start
  26.6 82.7 %reduce-scatter.2.cloned.1.call-done = f32[16,8,512]{2,1,0:T(8,128)} async-done(((f32[256,8,512]{2,1,0:T(8,128)}), f32[16,8,512]{2,1,0:T(8,128)}) %reduce-scatter.2.cloned.1.call-update) | async-done | bytes 262160 | tf_op jit(solution)/shard_map/reduce_scatter | solution.py:44
  109.4 10.2 %all_to_all.18 = f32[16,8,512]{2,1,0:T(8,128)S(1)} all-to-all(f32[16,8,512]{2,1,0:T(8,128)} %reduce-scatter.2.cloned.1.call-done), channel_id=1, replica_groups=mesh['depth'=16,'coef'=8] {'coef'}, dimensions={0} | all-to-all | bytes 524288 | tf_op jit(solution)/shard_map/all_to_all | solution.py:47
  119.5 1.0 fusion.10
  120.5 0.0 all-gather.2.cloned.1.call-update
  120.6 323.8 %all-gather.2.cloned.1.call-done = bf16[256,64,512]{2,1,0:T(8,128)(2,1)} async-done(((bf16[2,64,512]{2,1,0:T(8,128)(2,1)}), bf16[256,64,512]{2,1,0:T(8,128)(2,1)}) %all-gather.2.cloned.1.call-update) | async-done | bytes 16777232 | tf_op jit(solution)/shard_map/all_gather | solution.py:58
  444.3 8.0 %fusion.3 = bf16[256,8,512]{2,1,0:T(8,128)(2,1)S(1)} fusion(bf16[256,64,512]{2,1,0:T(8,128)(2,1)} %all-gather.2.cloned.1.call-done, bf16[64,64]{1,0:T(8,128)(2,1)S(1)} %copy-done, s32[]{:T(128)S(6)} %select_n.10), kind=kOutput, calls=%fused_computation.17 | convolution fusion | flops 136314880 | bytes 18876420 | tf_op jit(solution)/shard_map/ygx,kg->ykx/dot_general | solution.py:56
  452.4 1.6 convert_bitcast_fusion.2
  454.0 1.6 convert_bitcast_fusion.1
  455.5 1.6 convert_bitcast_fusion
  457.1 1.6 convert_bitcast_fusion.3
  458.7 3.9 pad_maximum_fusion
  462.5 11.6 %copy.42 = bf16[4,256,8,512]{3,2,1,0:T(8,128)(2,1)} copy(bf16[4,256,8,512]{3,1,2,0:T(8,128)(2,1)} %pad_maximum_fusion) | data formatting | bytes 16777216
  (8 shorter events, 0.0 us)
Async XLA Ops:
  7.2 112.4 %copy-start = (bf16[64,64]{1,0:T(8,128)(2,1)S(1)}, bf16[64,64]{1,0:T(8,128)(2,1)}, u32[]{:S(2)}) copy-start(bf16[64,64]{1,0:T(8,128)(2,1)} %param.9) | copy-start | bytes 24580
  7.2 102.2 %reduce-scatter.2.cloned.1.call-start = ((), (), s32[]{:S(2)}) async-start(), calls=%async_computation.2 | async-start | bytes 4456448 | tf_op jit(solution)/shard_map/reduce_scatter | solution.py:44
  26.6 93.0 %copy-start.2 = (f32[2,64,512]{2,1,0:T(8,128)S(1)}, f32[2,64,512]{2,1,0:T(8,128)}, u32[]{:S(2)}) copy-start(f32[2,64,512]{2,1,0:T(8,128)} %param.10) | copy-start | bytes 786436
  26.6 93.0 %copy-start.3 = (s32[2,64,512]{2,1,0:T(8,128)S(1)}, s32[2,64,512]{2,1,0:T(8,128)}, u32[]{:S(2)}) copy-start(s32[2,64,512]{2,1,0:T(8,128)} %param.11) | copy-start | bytes 786436
  26.6 417.8 %all-gather.2.cloned.1.call-start = ((), (), s32[]{:S(2)}) async-start(), calls=%async_computation.3 | async-start | bytes 16908288 | tf_op jit(solution)/shard_map/all_gather | solution.py:58
  462.5 11.6 %copy-start.1 = (bf16[64,64]{1,0:T(8,128)(2,1)S(1)}, bf16[64,64]{1,0:T(8,128)(2,1)}, u32[]{:S(2)}) copy-start(bf16[64,64]{1,0:T(8,128)(2,1)} %param.9) | copy-start | bytes 24580
Sparse Core Ops, SparseCore 0:
  26.7 82.6 reduce-scatter.1
  120.7 323.6 all-gather.1
where the time goes:
time: 481 us
  waiting for transfers between devices  407 us (85%)
  matrix products  22.9 us (5%)
  local copies, waits for them, and re-layouts  21 us (4%)
  between operations  14.1 us (3%)
  blocking collectives  10.2 us (2%)
  other arithmetic  6.2 us (1%)
    all_gather x1, waiting for transfers between devices, shards(): lax.all_gather(residual, ('depth', 'coef'), axis=0, tiled=True)  324 us
    reduce_scatter x1, waiting for transfers between devices, shards(): lax.psum_scatter(project_rows(volume, interp), 'depth', scatter_dimension...  82.7 us
    unnamed x9, local copies, waits for them, and re-layouts  11.6 us
    all_to_all x1, blocking collectives, shards(): lax.all_to_all(owned_rows, 'coef', split_axis=0, concat_axis=1, tiled=True)  10.2 us
  transfers between devices with their start and end apart: 2, of which 2 were waited for; matrix products, arithmetic and copies ran while one was open for 0% of the time, Pallas kernels for 0%

commit v1 on v0

v1 whole, which is shorter than its diff:
```python
import functools

import jax
import jax.numpy as jnp
from jax import lax
from jax.experimental import pallas as pl
from jax.experimental.pallas import tpu as pltpu
from jax.sharding import PartitionSpec as P

MESH = pl.DeviceIdType.MESH
X = 512
LOCAL = 4
COEF = 8
BLOCK = 256
HALF = 128
PIECE = 16
ORDER = ((1, 0), (0, 1), (2, 0), (3, 1), (1, 1), (0, 0), (2, 1), (3, 0))


def place():
    d = lax.axis_index("depth")
    c = lax.axis_index("coef")
    return c % 4, c // 4, (d // 2) % 2, d // 4, d % 2


def device(x, yl, yh, z, core):
    return {"depth": z * 4 + yh * 2 + core, "coef": yl * 4 + x}


def exchange(
    vol, shift, frac, basis, basis_t, data, mask,
    grad_rows, resid,
    volbuf, interp, part, theirs, outgoing, incoming, total, wanted, valid, gp, gathered, res_buf,
    vol_sem, in_sem, pair_send, pair_recv, send_sem, recv_sem, back_send, back_recv,
    share_send, share_recv, out_sem,
):
    x, yl, yh, z, core = place()
    mine = yl * 4 + x
    partner = device(x, yl, yh, z, 1 - core)

    barrier = pltpu.get_barrier_semaphore()
    pl.semaphore_signal(barrier, inc=1, device_id=partner, device_id_type=MESH)
    for dz in range(4):
        for dyh in range(2):
            for dyl in range(2):
                for dx in range(4):
                    if dz or dyh or dyl or dx:
                        pl.semaphore_signal(
                            barrier,
                            inc=1,
                            device_id=device((x + dx) % 4, yl ^ dyl, yh ^ dyh, (z + dz) % 4, core),
                            device_id_type=MESH,
                        )

    loads = []
    for i, (dz, dyh) in enumerate(ORDER):
        block = ((z + dz) % 4) * 2 + (yh ^ dyh)
        load = pltpu.make_async_copy(
            vol.at[:, pl.ds(pl.multiple_of(block * BLOCK, BLOCK), BLOCK)], volbuf.at[i], vol_sem.at[i]
        )
        load.start()
        loads.append(load)
    load_data = pltpu.make_async_copy(data, wanted, in_sem.at[0])
    load_mask = pltpu.make_async_copy(mask, valid, in_sem.at[1])
    load_data.start()
    load_mask.start()

    for layer in range(LOCAL):
        s = shift[layer]
        w = frac[layer].astype(jnp.float32) * 0.0625

        def fill(t, carry, layer=layer, s=s, w=w):
            rows = t * HALF + lax.broadcasted_iota(jnp.int32, (HALF, X), 0)
            cols = lax.broadcasted_iota(jnp.int32, (HALF, X), 1)
            gap = cols - rows - s
            tile = jnp.where(gap == 0, 1.0 - w, jnp.where(gap == 1, w, 0.0))
            interp[layer, pl.ds(pl.multiple_of(t * HALF, HALF), HALF)] = tile.astype(jnp.bfloat16)
            return carry

        lax.fori_loop(0, X // HALF, fill, 0)

    for i in range(8):
        loads[i].wait()
        running = None
        for layer in range(LOCAL):
            slab = jnp.dot(volbuf[i, layer], interp[layer], preferred_element_type=jnp.float32)
            running = slab if running is None else running + slab
        part[i, 0] = running[:HALF]
        part[i, 1] = running[HALF:]

    pl.semaphore_wait(barrier, 64)

    shares = []
    for i in range(8):
        share = pltpu.make_async_remote_copy(
            part.at[i, 1 - core], theirs.at[i], pair_send.at[i], pair_recv.at[i],
            device_id=partner, device_id_type=MESH,
        )
        share.start()
        shares.append(share)

    load_data.wait()
    load_mask.wait()

    for i, (dz, dyh) in enumerate(ORDER):
        shares[i].wait_recv()
        outgoing[i] = (part[i, core] + theirs[i]).astype(jnp.bfloat16)
        for dyl in range(2):
            for dx in range(4):
                tyl, tx = yl ^ dyl, (x + dx) % 4
                source = outgoing.at[i, pl.ds(pl.multiple_of((tyl * 4 + tx) * PIECE, PIECE), PIECE)]
                target = incoming.at[i, pl.ds(pl.multiple_of(mine * PIECE, PIECE), PIECE)]
                if dz or dyh or dyl or dx:
                    pltpu.make_async_remote_copy(
                        source, target, send_sem.at[i], recv_sem.at[i],
                        device_id=device(tx, tyl, yh ^ dyh, (z + dz) % 4, core), device_id_type=MESH,
                    ).start()
                else:
                    keep = pltpu.make_async_copy(source, target, in_sem.at[2])
                    keep.start()

    for i in range(8):
        if ORDER[i] == (0, 0):
            keep.wait()
            pltpu.make_async_remote_copy(
                outgoing.at[i, pl.ds(0, 7 * PIECE)], incoming.at[i, pl.ds(0, 7 * PIECE)],
                send_sem.at[i], recv_sem.at[i], device_id=partner, device_id_type=MESH,
            ).wait_recv()
        else:
            pltpu.make_async_remote_copy(
                outgoing.at[i], incoming.at[i], send_sem.at[i], recv_sem.at[i],
                device_id=partner, device_id_type=MESH,
            ).wait_recv()
        if i == 0:
            total[...] = incoming[i].astype(jnp.float32)
        else:
            total[...] += incoming[i].astype(jnp.float32)

    sums = total[...].reshape(COEF, 2, COEF, X)
    slabs = []
    for r in range(2):
        proj = sums[:, r].reshape(64, X)
        high = proj.astype(jnp.bfloat16)
        low = (proj - high.astype(jnp.float32)).astype(jnp.bfloat16)
        predicted = jnp.dot(basis_t[...], high, preferred_element_type=jnp.float32) + jnp.dot(
            basis_t[...], low, preferred_element_type=jnp.float32
        )
        residual = (valid[r].astype(jnp.float32) * (predicted - jnp.sqrt(wanted[r]))).astype(jnp.bfloat16)
        res_buf[r] = residual
        slab = 2.0 * jnp.dot(basis[...], residual, preferred_element_type=jnp.float32)
        slabs.append(slab.reshape(COEF, COEF, X))
    gp[...] = jnp.stack(slabs, axis=1).reshape(HALF, X).astype(jnp.bfloat16)

    own_row = pl.multiple_of((z * 64 + yh * 32 + core * 16 + yl * 8 + x * 2) * COEF, PIECE)
    for i, (dz, dyh) in enumerate(ORDER):
        for dyl in range(2):
            for dx in range(4):
                tyl, tx = yl ^ dyl, (x + dx) % 4
                source = gp.at[pl.ds(pl.multiple_of((tyl * 4 + tx) * PIECE, PIECE), PIECE)]
                target = gathered.at[pl.ds(own_row, PIECE)]
                if dz or dyh or dyl or dx:
                    pltpu.make_async_remote_copy(
                        source, target, back_send.at[i], back_recv.at[i],
                        device_id=device(tx, tyl, yh ^ dyh, (z + dz) % 4, core), device_id_type=MESH,
                    ).start()
                else:
                    keep = pltpu.make_async_copy(source, target, in_sem.at[2])
                    keep.start()
    store_res = pltpu.make_async_copy(res_buf, resid, in_sem.at[0])
    store_res.start()

    passes = []
    for i, (dz, dyh) in enumerate(ORDER):
        block = ((z + 4 - dz) % 4) * 2 + (yh ^ dyh)
        rows = gathered.at[pl.ds(pl.multiple_of(block * BLOCK + core * HALF, HALF), HALF)]
        if dz or dyh:
            pltpu.make_async_remote_copy(
                gp, rows, back_send.at[i], back_recv.at[i], device_id=partner, device_id_type=MESH
            ).wait_recv()
        else:
            keep.wait()
            pltpu.make_async_remote_copy(
                gp.at[pl.ds(0, 7 * PIECE)],
                gathered.at[pl.ds(pl.multiple_of(block * BLOCK + core * HALF, HALF), 7 * PIECE)],
                back_send.at[i], back_recv.at[i], device_id=partner, device_id_type=MESH,
            ).wait_recv()
        onward = pltpu.make_async_remote_copy(
            rows, rows, share_send.at[i], share_recv.at[i], device_id=partner, device_id_type=MESH
        )
        onward.start()
        passes.append(onward)
    stores = []
    for i, (dz, dyh) in enumerate(ORDER):
        block = ((z + 4 - dz) % 4) * 2 + (yh ^ dyh)
        passes[i].wait_recv()
        span = pl.ds(pl.multiple_of(block * BLOCK, BLOCK), BLOCK)
        store = pltpu.make_async_copy(gathered.at[span], grad_rows.at[span], out_sem.at[i])
        store.start()
        stores.append(store)

    for i in range(8):
        shares[i].wait_send()
        count = 7 * PIECE if ORDER[i] == (0, 0) else HALF
        pltpu.make_async_remote_copy(
            outgoing.at[i, pl.ds(0, count)], incoming.at[i, pl.ds(0, count)],
            send_sem.at[i], recv_sem.at[i], device_id=partner, device_id_type=MESH,
        ).wait_send()
        pltpu.make_async_remote_copy(
            gp.at[pl.ds(0, count)], gathered.at[pl.ds(0, count)],
            back_send.at[i], back_recv.at[i], device_id=partner, device_id_type=MESH,
        ).wait_send()
        passes[i].wait_send()
    for store in stores:
        store.wait()
    store_res.wait()


def back_project(shift, frac, rows_ref, res_ref, grad_ref, res_out, interp):
    @pl.when(pl.program_id(0) == 0)
    def _():
        res_out[...] = res_ref[...]
        for layer in range(LOCAL):
            s = shift[layer]
            w = frac[layer].astype(jnp.float32) * 0.0625

            def fill(t, carry, layer=layer, s=s, w=w):
                rows = t * HALF + lax.broadcasted_iota(jnp.int32, (HALF, X), 0)
                cols = lax.broadcasted_iota(jnp.int32, (HALF, X), 1)
                gap = rows - cols - s
                tile = jnp.where(gap == 0, 1.0 - w, jnp.where(gap == 1, w, 0.0))
                interp[layer, pl.ds(pl.multiple_of(t * HALF, HALF), HALF)] = tile.astype(jnp.bfloat16)
                return carry

            lax.fori_loop(0, X // HALF, fill, 0)

    for layer in range(LOCAL):
        grad_ref[layer] = jnp.dot(
            rows_ref[...], interp[layer], preferred_element_type=jnp.float32
        ).astype(jnp.bfloat16)


def shards(volume, shift, frac, basis, data, mask):
    layers, rows, coefs, cols = volume.shape
    flat = rows * coefs
    vmem = pl.BlockSpec(memory_space=pltpu.VMEM)
    smem = pl.BlockSpec(memory_space=pltpu.SMEM)
    hbm = pl.BlockSpec(memory_space=pl.ANY)
    dma = pltpu.SemaphoreType.DMA
    grad_rows, resid = pl.pallas_call(
        exchange,
        out_shape=(
            jax.ShapeDtypeStruct((flat, cols), jnp.bfloat16),
            jax.ShapeDtypeStruct(data.shape, jnp.bfloat16),
        ),
        in_specs=[hbm, smem, smem, vmem, vmem, hbm, hbm],
        out_specs=(hbm, hbm),
        scratch_shapes=[
            pltpu.VMEM((8, layers, BLOCK, cols), jnp.bfloat16),
            pltpu.VMEM((layers, cols, cols), jnp.bfloat16),
            pltpu.VMEM((8, 2, HALF, cols), jnp.float32),
            pltpu.VMEM((8, HALF, cols), jnp.float32),
            pltpu.VMEM((8, HALF, cols), jnp.bfloat16),
            pltpu.VMEM((8, HALF, cols), jnp.bfloat16),
            pltpu.VMEM((HALF, cols), jnp.float32),
            pltpu.VMEM(data.shape, jnp.float32),
            pltpu.VMEM(mask.shape, jnp.int32),
            pltpu.VMEM((HALF, cols), jnp.bfloat16),
            pltpu.VMEM((flat, cols), jnp.bfloat16),
            pltpu.VMEM(data.shape, jnp.bfloat16),
            dma((8,)), dma((3,)), dma((8,)), dma((8,)), dma((8,)), dma((8,)), dma((8,)), dma((8,)),
            dma((8,)), dma((8,)), dma((8,)),
        ],
        compiler_params=pltpu.CompilerParams(
            collective_id=0, has_side_effects=True, vmem_limit_bytes=60 * 1024 * 1024
        ),
        name="exchange",
    )(volume.reshape(layers, flat, cols), shift, frac, basis, basis.T, data, mask)
    gradient, residual = pl.pallas_call(
        back_project,
        grid=(flat // BLOCK,),
        out_shape=(
            jax.ShapeDtypeStruct((layers, flat, cols), jnp.bfloat16),
            jax.ShapeDtypeStruct(data.shape, jnp.bfloat16),
        ),
        in_specs=[smem, smem, pl.BlockSpec((BLOCK, cols), lambda i: (i, 0)), pl.BlockSpec(data.shape, lambda i: (0, 0, 0))],
        out_specs=(
            pl.BlockSpec((layers, BLOCK, cols), lambda i: (0, i, 0)),
            pl.BlockSpec(data.shape, lambda i: (0, 0, 0)),
        ),
        scratch_shapes=[pltpu.VMEM((layers, cols, cols), jnp.bfloat16)],
        compiler_params=pltpu.CompilerParams(vmem_limit_bytes=24 * 1024 * 1024),
        name="back_project",
    )(shift, frac, grad_rows, resid)
    return gradient.reshape(volume.shape), residual


def solution(mesh):
    in_specs = (
        P("depth", None, "coef", None),
        P("depth"),
        P("depth"),
        P(),
        P(("depth", "coef"), None, None),
        P(("depth", "coef"), None, None),
    )
    out_specs = (P("depth", None, "coef", None), P(("depth", "coef"), None, None))
    return jax.shard_map(shards, mesh=mesh, in_specs=in_specs, out_specs=out_specs, check_vma=False)
```

time: 481 us -> 64.9 us (0.13)
  waiting for transfers between devices: 407 us -> 0 us
  Pallas kernels: 0 us -> 60 us
  matrix products: 22.9 us -> 0 us
  local copies, waits for them, and re-layouts: 21 us -> 3.92 us
  between operations: 14.1 us -> 0.68 us
  blocking collectives: 10.2 us -> 0 us
  other arithmetic: 6.2 us -> 0 us
    all_gather x1 -> x0, waiting for transfers between devices: 324 us -> none  [shards(): lax.all_gather(residual, ('depth', 'coef'), axis=0, tiled=True)]
    reduce_scatter x1 -> x0, waiting for transfers between devices: 82.7 us -> none  [shards(): lax.psum_scatter(project_rows(volume, interp), 'depth', scatter_dimension...]
    pallas_call x0 -> x2, Pallas kernels: none -> 60 us  [the longest x1 51 us: shards(): pl.pallas_call(exchange, out_shape=(jax.ShapeDtypeStruct((flat, cols), jn...]
    dot_general x10 -> x0, matrix products: 22.9 us -> none  [the longest x1 8.04 us: shards(): jnp.einsum('ygx,kg->ykx', lax.all_gather(residual, ('depth', 'coef'), axi...]
    all_to_all x1 -> x0, blocking collectives: 10.2 us -> none  [shards(): lax.all_to_all(owned_rows, 'coef', split_axis=0, concat_axis=1, tiled=True)]
    unnamed x9, local copies, waits for them, and re-layouts: 11.6 us -> 3.92 us
    add x1 -> x0, local copies, waits for them, and re-layouts: 5.56 us -> none  [project_rows(): running = slab if running is None else running + slab]
  transfers between devices with their start and end apart: 2 -> 0, of which waited for: 2 -> 0; matrix products, arithmetic and copies ran while one was open for 0% -> 0% of each run, Pallas kernels for 0% -> 0%
where the time goes in v1:
time: 64.9 us; the launch traced here: 64.6 us
  Pallas kernels  60 us (92%)
  local copies, waits for them, and re-layouts  3.92 us (6%)
  between operations  0.68 us (1%)
    pallas_call x1, Pallas kernels, shards(): pl.pallas_call(exchange, out_shape=(jax.ShapeDtypeStruct((flat, cols), jn...  51 us
    pallas_call x1, Pallas kernels, shards(): pl.pallas_call(back_project, grid=(flat // BLOCK,), out_shape=(jax.ShapeD...  9.05 us
    unnamed x9, local copies, waits for them, and re-layouts  3.92 us

profile of v1, /device:TPU:1, one launch (start us, length us, event | category | flops | bytes accessed | tf_op | source)
XLA Modules:
  0.0 64.6 jit_solution(3317320375421575217)
XLA Ops:
  0.6 0.0 copy-start.3
  0.6 0.0 copy-start.2
  0.7 1.4 %copy.8 = bf16[64,64]{0,1:T(8,128)(2,1)} copy(bf16[64,64]{1,0:T(8,128)(2,1)} %basis.1) | data formatting | bytes 16384 | tf_op args[3]
  2.1 51.0 %exchange.1 = (bf16[2048,512]{1,0:T(8,128)(2,1)}, bf16[2,64,512]{2,1,0:T(8,128)(2,1)}) custom-call(bf16[4,2048,512]{2,1,0:T(8,128)(2,1)} %bitcast.3, s32[4]{0:T(128)} %shift.3, s32[4]{0:T(128)} %frac.3, bf16[64,64]{1,0:T(8,128)(2,1)} %basis.1, bf16[64,64]{1,0:T(8,128)(2,1)} %bitcast.4, f32[2,64,512]{2,1,0:T(8,128)} %data.1, s32[2,64,512]{2,1,0:T(8,128)} %mask.1), custom_call_target="tpu_custom_call" | custom-call | tf_op jit(solution)/shard_map/exchange/pallas_call | solution.py:249
  53.0 0.0 copy-done.3
  53.0 0.0 copy-done.2
  53.0 0.0 copy-start
  53.1 1.6 %copy-done = bf16[2048,512]{1,0:T(8,128)(2,1)S(1)} copy-done((bf16[2048,512]{1,0:T(8,128)(2,1)S(1)}, bf16[2048,512]{1,0:T(8,128)(2,1)}, u32[]{:S(2)}) %copy-start) | copy-done | bytes 2097176
  54.6 0.0 copy-start.1
  54.6 0.9 %copy-done.1 = bf16[2,64,512]{2,1,0:T(8,128)(2,1)S(1)} copy-done((bf16[2,64,512]{2,1,0:T(8,128)(2,1)S(1)}, bf16[2,64,512]{2,1,0:T(8,128)(2,1)}, u32[]{:S(2)}) %copy-start.1) | copy-done | bytes 131096
  55.5 9.0 %back_project.1 = (bf16[4,2048,512]{2,1,0:T(8,128)(2,1)}, bf16[2,64,512]{2,1,0:T(8,128)(2,1)}) custom-call(s32[4]{0:T(128)S(1)} %copy-done.2, s32[4]{0:T(128)S(1)} %copy-done.3, bf16[2048,512]{1,0:T(8,128)(2,1)S(1)} %copy-done, bf16[2,64,512]{2,1,0:T(8,128)(2,1)S(1)} %copy-done.1), custom_call_target="tpu_custom_call" | custom-call | tf_op jit(solution)/shard_map/back_project/pallas_call | solution.py:278
Async XLA Ops:
  0.6 52.4 %copy-start.3 = (s32[4]{0:T(128)S(1)}, s32[4]{0:T(128)}, u32[]{:S(2)}) copy-start(s32[4]{0:T(128)} %frac.3) | copy-start | bytes 52
  0.6 52.4 %copy-start.2 = (s32[4]{0:T(128)S(1)}, s32[4]{0:T(128)}, u32[]{:S(2)}) copy-start(s32[4]{0:T(128)} %shift.3) | copy-start | bytes 52
  53.0 1.6 %copy-start = (bf16[2048,512]{1,0:T(8,128)(2,1)S(1)}, bf16[2048,512]{1,0:T(8,128)(2,1)}, u32[]{:S(2)}) copy-start(bf16[2048,512]{1,0:T(8,128)(2,1)} %get-tuple-element.6.rows_ref) | copy-start | bytes 6291460
  54.6 0.9 %copy-start.1 = (bf16[2,64,512]{2,1,0:T(8,128)(2,1)S(1)}, bf16[2,64,512]{2,1,0:T(8,128)(2,1)}, u32[]{:S(2)}) copy-start(bf16[2,64,512]{2,1,0:T(8,128)(2,1)} %get-tuple-element.7.res_ref) | copy-start | bytes 393220

commit v2 on v0

v2 whole, which is shorter than its diff:
```python
import functools

import jax
import jax.numpy as jnp
from jax import lax
from jax.experimental import pallas as pl
from jax.experimental.pallas import tpu as pltpu
from jax.sharding import PartitionSpec as P

MESH = pl.DeviceIdType.MESH
X = 512
LOCAL = 4
COEF = 8
BLOCK = 256
HALF = 128
PEERS = sorted(
    ((dz, dyh, dyl, dx) for dz in range(4) for dyh in range(2) for dyl in range(2) for dx in range(4))
)[:0:-1]
GROUPS = ((0, 4), (4, 2), (6, 2))
VMEM = 60 * 1024 * 1024
PIECES = 2
ORDER = ((1, 0), (0, 1), (2, 0), (3, 1), (1, 1), (0, 0), (2, 1), (3, 0))


def place():
    d = lax.axis_index("depth")
    c = lax.axis_index("coef")
    return c % 4, c // 4, (d // 2) % 2, d // 4, d % 2


def device(x, yl, yh, z, core):
    return {"depth": z * 4 + yh * 2 + core, "coef": yl * 4 + x}


def table(layer, shift, frac, band, corner, forward):
    s = shift[layer]
    w = frac[layer].astype(jnp.float32) * 0.0625
    rows = lax.broadcasted_iota(jnp.int32, (BLOCK, BLOCK), 0)
    cols = lax.broadcasted_iota(jnp.int32, (BLOCK, BLOCK), 1)
    gap = (cols - rows if forward else rows - cols) - s
    tile = jnp.where(gap == 0, 1.0 - w, jnp.where(gap == 1, w, 0.0)).astype(jnp.bfloat16)
    empty = jnp.zeros((HALF, HALF), jnp.bfloat16)
    span = pl.ds(layer * BLOCK, BLOCK)
    band[span] = tile
    corner[span] = jnp.concatenate(
        [
            jnp.concatenate([empty, tile[:HALF, HALF:]], axis=1),
            jnp.concatenate([tile[HALF:, :HALF], empty], axis=1),
        ],
        axis=0,
    )


def banded(lanes, band, corner):
    low, middle, high = lanes(0), lanes(HALF), lanes(BLOCK)
    m = low.shape[0]
    sides = jnp.dot(jnp.concatenate([low, high], axis=0), band, preferred_element_type=jnp.float32)
    inner = jnp.dot(middle, corner, preferred_element_type=jnp.float32)
    return (
        sides[:m, :HALF],
        sides[:m, HALF:] + inner[:, :HALF],
        sides[m:, :HALF] + inner[:, HALF:],
        sides[m:, HALF:],
    )


def exchange(
    vol, shift_hbm, frac_hbm, basis, data, mask,
    grad_rows, tables, resid,
    volbuf, shift, frac, band, corner, back_band, back_corner, gathered, res_buf, part, theirs, outgoing, incoming, total, wanted, valid, mix, gp,
    vol_sem, in_sem, self_sem, pair_send, pair_recv, send_sem, recv_sem, back_send, back_recv,
    share_send, share_recv, out_sem,
):
    x, yl, yh, z, core = place()
    mine = yl * 4 + x
    partner = device(x, yl, yh, z, 1 - core)

    def remote(source, target, send, recv, to=partner):
        return pltpu.make_async_remote_copy(source, target, send, recv, device_id=to, device_id_type=MESH)

    words = [
        pltpu.make_async_copy(shift_hbm, shift, in_sem.at[3]),
        pltpu.make_async_copy(frac_hbm, frac, in_sem.at[4]),
    ]
    for load in words:
        load.start()
    loads = []
    for i, (dz, dyh) in enumerate(ORDER):
        block = ((z + dz) % 4) * 2 + (yh ^ dyh)
        load = pltpu.make_async_copy(
            vol.at[:, pl.ds(pl.multiple_of(block * BLOCK, BLOCK), BLOCK)], volbuf.at[i], vol_sem.at[i]
        )
        load.start()
        loads.append(load)
    barrier = pltpu.get_barrier_semaphore()
    for dz, dyh, dyl, dx in PEERS:
        to = device((x + dx) % 4, yl ^ dyl, yh ^ dyh, (z + dz) % 4, core)
        pl.semaphore_signal(barrier, inc=1, device_id=to, device_id_type=MESH)
    pl.semaphore_signal(barrier, inc=1, device_id=partner, device_id_type=MESH)

    small = [
        pltpu.make_async_copy(data, wanted, in_sem.at[0]),
        pltpu.make_async_copy(mask, valid, in_sem.at[1]),
        pltpu.make_async_copy(basis, mix, in_sem.at[2]),
    ]
    for load in small:
        load.start()

    for load in words:
        load.wait()
    for layer in range(LOCAL):
        table(layer, shift, frac, band, corner, True)

    def compute(first, count):
        for i in range(first, first + count):
            loads[i].wait()

        def lanes(low):
            return jnp.concatenate(
                [
                    volbuf[first : first + count, layer, :, low : low + BLOCK].reshape(count * BLOCK, BLOCK)
                    for layer in range(LOCAL)
                ],
                axis=1,
            )

        for q, piece in enumerate(banded(lanes, band[...], corner[...])):
            part[first : first + count, :, :, :, :, q * HALF : (q + 1) * HALF] = piece.reshape(
                count, 2, COEF, 2, COEF, HALF
            )

    shares = [remote(part.at[i, 1 - core], theirs.at[i], pair_send.at[i], pair_recv.at[i]) for i in range(8)]

    def is_self(i, dyl, dx):
        return ORDER[i] == (0, 0) and dyl == 0 and dx == 0

    def dispatch(r, i):
        dz, dyh = ORDER[i]
        if r == 0:
            shares[i].wait_recv()
        outgoing[r, i] = (part[i, core, :, r] + theirs[i, :, r]).astype(jnp.bfloat16)
        for dyl in range(2):
            for dx in range(4):
                tyl, tx = yl ^ dyl, (x + dx) % 4
                source = outgoing.at[r, i, tyl * 4 + tx]
                target = incoming.at[r, i, mine]
                if is_self(i, dyl, dx):
                    pltpu.make_async_copy(source, target, self_sem.at[r]).start()
                else:
                    to = device(tx, tyl, yh ^ dyh, (z + dz) % 4, core)
                    remote(source, target, send_sem.at[r, i], recv_sem.at[r, i], to).start()

    done, ready = 0, 0
    for first, count in GROUPS:
        compute(first, count)
        if first == 0:
            pl.semaphore_wait(barrier, 64)
        for i in range(first, first + count):
            shares[i].start()
        while done < ready:
            dispatch(0, done)
            done += 1
        ready = first + count
    while done < 8:
        dispatch(0, done)
        done += 1
    for i in range(8):
        dispatch(1, i)

    for layer in range(LOCAL):
        table(layer, shift, frac, back_band, back_corner, False)
    store_tables = [
        pltpu.make_async_copy(back_band, tables.at[0], in_sem.at[3]),
        pltpu.make_async_copy(back_corner, tables.at[1], in_sem.at[4]),
    ]
    for store in store_tables:
        store.start()
    for load in small:
        load.wait()
    turned = mix[...].astype(jnp.float32).T.astype(jnp.bfloat16)

    for r in range(2):
        for i in range(8):
            count = 8
            if ORDER[i] == (0, 0):
                pltpu.make_async_copy(outgoing.at[r, i, 0], incoming.at[r, i, 0], self_sem.at[r]).wait()
                count = 7
            remote(
                outgoing.at[r, i, pl.ds(0, count)], incoming.at[r, i, pl.ds(0, count)],
                send_sem.at[r, i], recv_sem.at[r, i],
            ).wait_recv()
            piece = incoming[r, i].astype(jnp.float32).reshape(64, X)
            if i == 0:
                total[r] = piece
            else:
                total[r] += piece
        proj = total[r]
        high = proj.astype(jnp.bfloat16)
        low = (proj - high.astype(jnp.float32)).astype(jnp.bfloat16)
        predicted = jnp.dot(turned, high, preferred_element_type=jnp.float32) + jnp.dot(
            turned, low, preferred_element_type=jnp.float32
        )
        residual = (valid[r].astype(jnp.float32) * (predicted - jnp.sqrt(wanted[r]))).astype(jnp.bfloat16)
        res_buf[r] = residual
        slab = 2.0 * jnp.dot(mix[...], residual, preferred_element_type=jnp.float32)
        gp[r] = slab.reshape(COEF, COEF, X).astype(jnp.bfloat16)
        for i, (dz, dyh) in enumerate(ORDER):
            for dyl in range(2):
                for dx in range(4):
                    tyl, tx = yl ^ dyl, (x + dx) % 4
                    source = gp.at[r, tyl * 4 + tx]
                    target = gathered.at[z * 2 + yh, mine, r]
                    if is_self(i, dyl, dx):
                        pltpu.make_async_copy(source, target, self_sem.at[r]).start()
                    else:
                        to = device(tx, tyl, yh ^ dyh, (z + dz) % 4, core)
                        remote(source, target, back_send.at[r, i], back_recv.at[r, i], to).start()

    store_res = pltpu.make_async_copy(res_buf, resid, in_sem.at[0])
    store_res.start()
    passes = []
    for r in range(2):
        for i, (dz, dyh) in enumerate(ORDER):
            block = ((z + 4 - dz) % 4) * 2 + (yh ^ dyh)
            rows = gathered.at[block, :, r]
            count = 8
            if ORDER[i] == (0, 0):
                pltpu.make_async_copy(gp.at[r, 0], gathered.at[block, 0, r], self_sem.at[r]).wait()
                count = 7
            remote(
                gp.at[r, pl.ds(0, count)], gathered.at[block, pl.ds(0, count), r],
                back_send.at[r, i], back_recv.at[r, i],
            ).wait_recv()
            home = grad_rows.at[block, core, :, r]
            onward = remote(rows, home, share_send.at[r, i], share_recv.at[r, i])
            onward.start()
            store = pltpu.make_async_copy(rows, home, out_sem.at[r, i])
            store.start()
            passes += [onward, store]
    for store in passes + store_tables + [store_res]:
        store.wait()
    for i in range(8):
        shares[i].wait_send()
        count = 7 if ORDER[i] == (0, 0) else 8
        for r in range(2):
            remote(
                outgoing.at[r, i, pl.ds(0, count)], incoming.at[r, i, pl.ds(0, count)],
                send_sem.at[r, i], recv_sem.at[r, i],
            ).wait_send()
            remote(
                gp.at[r, pl.ds(0, count)], incoming.at[r, i, pl.ds(0, count)],
                back_send.at[r, i], back_recv.at[r, i],
            ).wait_send()


def back_project(rows_hbm, tables_hbm, res_in, grad, res_out, rows_ref, tables, res_buf, staged, load_sem, sem):
    size = rows_ref.shape[1]
    loads = [pltpu.make_async_copy(tables_hbm, tables, load_sem.at[0])]
    for t in range(PIECES):
        loads.append(pltpu.make_async_copy(rows_hbm.at[pl.ds(t * size, size)], rows_ref.at[t], load_sem.at[t + 1]))
    last = pltpu.make_async_copy(res_in, res_buf, load_sem.at[PIECES + 1])
    for load in loads + [last]:
        load.start()
    loads[0].wait()
    stores = []
    for t in range(PIECES):
        loads[t + 1].wait()
        for layer in range(LOCAL):
            span = slice(layer * BLOCK, (layer + 1) * BLOCK)
            pieces = banded(lambda low: rows_ref[t, :, low : low + BLOCK], tables[0, span], tables[1, span])
            for q, piece in enumerate(pieces):
                staged[t, layer, :, q * HALF : (q + 1) * HALF] = piece.astype(jnp.bfloat16)
            store = pltpu.make_async_copy(
                staged.at[t, layer], grad.at[layer, pl.ds(t * size, size)], sem.at[t * LOCAL + layer]
            )
            store.start()
            stores.append(store)
        if t == 0:
            last.wait()
            keep = pltpu.make_async_copy(res_buf, res_out, load_sem.at[0])
            keep.start()
            stores.append(keep)
    for store in stores:
        store.wait()


def shards(volume, shift, frac, basis, data, mask):
    layers, rows, coefs, cols = volume.shape
    flat = rows * coefs
    hbm = pl.BlockSpec(memory_space=pl.ANY)
    dma = pltpu.SemaphoreType.DMA
    tall = layers * BLOCK
    grad_rows, tables, resid = pl.pallas_call(
        exchange,
        out_shape=(
            jax.ShapeDtypeStruct((8, 2, 8, 2, coefs, cols), jnp.bfloat16),
            jax.ShapeDtypeStruct((2, tall, BLOCK), jnp.bfloat16),
            jax.ShapeDtypeStruct(data.shape, jnp.bfloat16),
        ),
        in_specs=[hbm] * 6,
        out_specs=(hbm, hbm, hbm),
        scratch_shapes=[
            pltpu.VMEM((8, layers, BLOCK, cols), jnp.bfloat16),
            pltpu.SMEM(shift.shape, jnp.int32),
            pltpu.SMEM(frac.shape, jnp.int32),
            pltpu.VMEM((tall, BLOCK), jnp.bfloat16),
            pltpu.VMEM((tall, BLOCK), jnp.bfloat16),
            pltpu.VMEM((tall, BLOCK), jnp.bfloat16),
            pltpu.VMEM((tall, BLOCK), jnp.bfloat16),
            pltpu.VMEM((8, 8, 2, coefs, cols), jnp.bfloat16),
            pltpu.VMEM(data.shape, jnp.bfloat16),
            pltpu.VMEM((8, 2, 8, 2, coefs, cols), jnp.float32),
            pltpu.VMEM((8, 8, 2, coefs, cols), jnp.float32),
            pltpu.VMEM((2, 8, 8, coefs, cols), jnp.bfloat16),
            pltpu.VMEM((2, 8, 8, coefs, cols), jnp.bfloat16),
            pltpu.VMEM((2, 64, cols), jnp.float32),
            pltpu.VMEM(data.shape, jnp.float32),
            pltpu.VMEM(mask.shape, jnp.int32),
            pltpu.VMEM(basis.shape, jnp.bfloat16),
            pltpu.VMEM((2, 8, coefs, cols), jnp.bfloat16),
            dma((8,)), dma((5,)), dma((2,)), dma((8,)), dma((8,)), dma((2, 8)), dma((2, 8)),
            dma((2, 8)), dma((2, 8)), dma((2, 8)), dma((2, 8)), dma((2, 8)),
        ],
        compiler_params=pltpu.CompilerParams(collective_id=0, has_side_effects=True, vmem_limit_bytes=VMEM),
        name="exchange",
    )(volume.reshape(layers, flat, cols), shift, frac, basis, data, mask)
    gradient, residual = pl.pallas_call(
        back_project,
        out_shape=(
            jax.ShapeDtypeStruct((layers, flat, cols), jnp.bfloat16),
            jax.ShapeDtypeStruct(data.shape, jnp.bfloat16),
        ),
        in_specs=[hbm] * 3,
        out_specs=(hbm, hbm),
        scratch_shapes=[
            pltpu.VMEM((PIECES, flat // PIECES, cols), jnp.bfloat16),
            pltpu.VMEM((2, tall, BLOCK), jnp.bfloat16),
            pltpu.VMEM(data.shape, jnp.bfloat16),
            pltpu.VMEM((PIECES, layers, flat // PIECES, cols), jnp.bfloat16),
            dma((PIECES + 2,)),
            dma((PIECES * layers,)),
        ],
        compiler_params=pltpu.CompilerParams(vmem_limit_bytes=VMEM),
        name="back_project",
    )(grad_rows.reshape(flat, cols), tables, resid)
    return gradient.reshape(volume.shape), residual


def solution(mesh):
    in_specs = (
        P("depth", None, "coef", None),
        P("depth"),
        P("depth"),
        P(),
        P(("depth", "coef"), None, None),
        P(("depth", "coef"), None, None),
    )
    out_specs = (P("depth", None, "coef", None), P(("depth", "coef"), None, None))
    return jax.shard_map(shards, mesh=mesh, in_specs=in_specs, out_specs=out_specs, check_vma=False)
```

time: 481 us -> 49.3 us (0.10)
  waiting for transfers between devices: 407 us -> 0 us
  Pallas kernels: 0 us -> 48.5 us
  matrix products: 22.9 us -> 0 us
  local copies, waits for them, and re-layouts: 21 us -> 0 us
  between operations: 14.1 us -> 0.64 us
  blocking collectives: 10.2 us -> 0 us
  other arithmetic: 6.2 us -> 0 us
    all_gather x1 -> x0, waiting for transfers between devices: 324 us -> none  [shards(): lax.all_gather(residual, ('depth', 'coef'), axis=0, tiled=True)]
    reduce_scatter x1 -> x0, waiting for transfers between devices: 82.7 us -> none  [shards(): lax.psum_scatter(project_rows(volume, interp), 'depth', scatter_dimension...]
    pallas_call x0 -> x2, Pallas kernels: none -> 48.5 us  [the longest x1 42.1 us: shards(): pl.pallas_call(exchange, out_shape=(jax.ShapeDtypeStruct((8, 2, 8, 2, coe...]
    dot_general x10 -> x0, matrix products: 22.9 us -> none  [the longest x1 8.04 us: shards(): jnp.einsum('ygx,kg->ykx', lax.all_gather(residual, ('depth', 'coef'), axi...]
    unnamed x9 -> x0, local copies, waits for them, and re-layouts: 11.6 us -> none
    all_to_all x1 -> x0, blocking collectives: 10.2 us -> none  [shards(): lax.all_to_all(owned_rows, 'coef', split_axis=0, concat_axis=1, tiled=True)]
    add x1 -> x0, local copies, waits for them, and re-layouts: 5.56 us -> none  [project_rows(): running = slab if running is None else running + slab]
  transfers between devices with their start and end apart: 2 -> 0, of which waited for: 2 -> 0; matrix products, arithmetic and copies ran while one was open for 0% -> 0% of each run, Pallas kernels for 0% -> 0%
where the time goes in v2:
time: 49.3 us; the launch traced here: 49.2 us
  Pallas kernels  48.5 us (98%)
  between operations  0.64 us (1%)
    pallas_call x1, Pallas kernels, shards(): pl.pallas_call(exchange, out_shape=(jax.ShapeDtypeStruct((8, 2, 8, 2, coe...  42.1 us
    pallas_call x1, Pallas kernels, shards(): pl.pallas_call(back_project, out_shape=(jax.ShapeDtypeStruct((layers, fla...  6.46 us

profile of v2, /device:TPU:1, one launch (start us, length us, event | category | flops | bytes accessed | tf_op | source)
XLA Modules:
  0.0 49.2 jit_solution(7361525895972385600)
XLA Ops:
  0.6 42.1 %exchange.1 = (bf16[8,2,8,2,8,512]{5,4,3,2,1,0:T(8,128)(2,1)}, bf16[2,1024,256]{2,1,0:T(8,128)(2,1)}, bf16[2,64,512]{2,1,0:T(8,128)(2,1)}) custom-call(bf16[4,2048,512]{2,1,0:T(8,128)(2,1)} %bitcast.3, s32[4]{0:T(128)} %shift_hbm.1, s32[4]{0:T(128)} %frac_hbm.1, bf16[64,64]{1,0:T(8,128)(2,1)} %basis.1, f32[2,64,512]{2,1,0:T(8,128)} %data.1, s32[2,64,512]{2,1,0:T(8,128)} %mask.1), custom_call_target="tpu_custom_call" | custom-call | tf_op jit(solution)/shard_map/exchange/pallas_call | solution.py:293
  42.7 6.5 %back_project.1 = (bf16[4,2048,512]{2,1,0:T(8,128)(2,1)}, bf16[2,64,512]{2,1,0:T(8,128)(2,1)}) custom-call(bf16[2048,512]{1,0:T(8,128)(2,1)} %bitcast.4, bf16[2,1024,256]{2,1,0:T(8,128)(2,1)} %get-tuple-element.8.tables_hbm, bf16[2,64,512]{2,1,0:T(8,128)(2,1)} %get-tuple-element.9.res_in), custom_call_target="tpu_custom_call" | custom-call | tf_op jit(solution)/shard_map/back_project/pallas_call | solution.py:327

commit v3 on v2

--- a/solution.py
+++ b/solution.py
@@ -14,12 +14,14 @@
 BLOCK = 256
 HALF = 128
 PEERS = sorted(
-    ((dz, dyh, dyl, dx) for dz in range(4) for dyh in range(2) for dyl in range(2) for dx in range(4))
+    ((dz, dyh, dyl, dx) for dz in range(4) for dyh in range(2) for dyl in range(2) for dx in range(4)),
+    key=lambda p: min(p[0], 4 - p[0]) + (1 if p[2] else 2 * p[1]) + min(p[3], 4 - p[3]),
 )[:0:-1]
 GROUPS = ((0, 4), (4, 2), (6, 2))
 VMEM = 60 * 1024 * 1024
-PIECES = 2
-ORDER = ((1, 0), (0, 1), (2, 0), (3, 1), (1, 1), (0, 0), (2, 1), (3, 0))
+PIECES = 4
+ORDER = ((1, 0), (0, 1), (2, 0), (3, 1), (1, 1), (2, 1), (3, 0), (0, 0))
+KEPT = tuple(7 if pair == (0, 0) else 8 for pair in ORDER)
 
 
 def place():
@@ -32,12 +34,12 @@
     return {"depth": z * 4 + yh * 2 + core, "coef": yl * 4 + x}
 
 
-def table(layer, shift, frac, band, corner, forward):
+def table(layer, shift, frac, band, corner):
     s = shift[layer]
     w = frac[layer].astype(jnp.float32) * 0.0625
     rows = lax.broadcasted_iota(jnp.int32, (BLOCK, BLOCK), 0)
     cols = lax.broadcasted_iota(jnp.int32, (BLOCK, BLOCK), 1)
-    gap = (cols - rows if forward else rows - cols) - s
+    gap = cols - rows - s
     tile = jnp.where(gap == 0, 1.0 - w, jnp.where(gap == 1, w, 0.0)).astype(jnp.bfloat16)
     empty = jnp.zeros((HALF, HALF), jnp.bfloat16)
     span = pl.ds(layer * BLOCK, BLOCK)
@@ -51,6 +53,18 @@
     )
 
 
+def back_table(shift, frac, pair):
+    rows = lax.broadcasted_iota(jnp.int32, (BLOCK, HALF), 0)
+    cols = lax.broadcasted_iota(jnp.int32, (BLOCK, HALF), 1)
+    halves = []
+    for layer in (2 * pair, 2 * pair + 1):
+        s = shift[layer]
+        w = frac[layer].astype(jnp.float32) * 0.0625
+        gap = rows - cols - jnp.where(s < 0, s + HALF, s)
+        halves.append(jnp.where(gap == 0, 1.0 - w, jnp.where(gap == 1, w, 0.0)).astype(jnp.bfloat16))
+    return jnp.concatenate(halves, axis=1)
+
+
 def banded(lanes, band, corner):
     low, middle, high = lanes(0), lanes(HALF), lanes(BLOCK)
     m = low.shape[0]
@@ -67,7 +81,7 @@
 def exchange(
     vol, shift_hbm, frac_hbm, basis, data, mask,
     grad_rows, tables, resid,
-    volbuf, shift, frac, band, corner, back_band, back_corner, gathered, res_buf, part, theirs, outgoing, incoming, total, wanted, valid, mix, gp,
+    volbuf, shift, frac, band, corner, back, gathered, res_buf, part, theirs, outgoing, incoming, total, wanted, valid, mix, gp,
     vol_sem, in_sem, self_sem, pair_send, pair_recv, send_sem, recv_sem, back_send, back_recv,
     share_send, share_recv, out_sem,
 ):
@@ -109,7 +123,7 @@
     for load in words:
         load.wait()
     for layer in range(LOCAL):
-        table(layer, shift, frac, band, corner, True)
+        table(layer, shift, frac, band, corner)
 
     def compute(first, count):
         for i in range(first, first + count):
@@ -167,14 +181,10 @@
     for i in range(8):
         dispatch(1, i)
 
-    for layer in range(LOCAL):
-        table(layer, shift, frac, back_band, back_corner, False)
-    store_tables = [
-        pltpu.make_async_copy(back_band, tables.at[0], in_sem.at[3]),
-        pltpu.make_async_copy(back_corner, tables.at[1], in_sem.at[4]),
-    ]
-    for store in store_tables:
-        store.start()
+    for pair in range(LOCAL // 2):
+        back[pair] = back_table(shift, frac, pair)
+    store_tables = pltpu.make_async_copy(back, tables, in_sem.at[3])
+    store_tables.start()
     for load in small:
         load.wait()
     turned = mix[...].astype(jnp.float32).T.astype(jnp.bfloat16)
@@ -218,8 +228,25 @@
 
     store_res = pltpu.make_async_copy(res_buf, resid, in_sem.at[0])
     store_res.start()
+    store_tables.wait()
+    for i in range(8):
+        shares[i].wait_send()
+        for r in range(2):
+            remote(
+                outgoing.at[r, i, pl.ds(0, KEPT[i])], incoming.at[r, i, pl.ds(0, KEPT[i])],
+                send_sem.at[r, i], recv_sem.at[r, i],
+            ).wait_send()
     passes = []
     for r in range(2):
+        if r == 1:
+            for i in range(8):
+                remote(
+                    gp.at[0, pl.ds(0, KEPT[i])], incoming.at[0, i, pl.ds(0, KEPT[i])],
+                    back_send.at[0, i], back_recv.at[0, i],
+                ).wait_send()
+            for store in passes:
+                store.wait()
+            passes = []
         for i, (dz, dyh) in enumerate(ORDER):
             block = ((z + 4 - dz) % 4) * 2 + (yh ^ dyh)
             rows = gathered.at[block, :, r]
@@ -237,47 +264,54 @@
             store = pltpu.make_async_copy(rows, home, out_sem.at[r, i])
             store.start()
             passes += [onward, store]
-    for store in passes + store_tables + [store_res]:
+    for store in passes + [store_res]:
         store.wait()
     for i in range(8):
-        shares[i].wait_send()
-        count = 7 if ORDER[i] == (0, 0) else 8
-        for r in range(2):
-            remote(
-                outgoing.at[r, i, pl.ds(0, count)], incoming.at[r, i, pl.ds(0, count)],
-                send_sem.at[r, i], recv_sem.at[r, i],
-            ).wait_send()
-            remote(
-                gp.at[r, pl.ds(0, count)], incoming.at[r, i, pl.ds(0, count)],
-                back_send.at[r, i], back_recv.at[r, i],
-            ).wait_send()
-
-
-def back_project(rows_hbm, tables_hbm, res_in, grad, res_out, rows_ref, tables, res_buf, staged, load_sem, sem):
+        remote(
+            gp.at[1, pl.ds(0, KEPT[i])], incoming.at[1, i, pl.ds(0, KEPT[i])], back_send.at[1, i], back_recv.at[1, i]
+        ).wait_send()
+
+
+def back_project(
+    rows_hbm, tables_hbm, res_in, shift_hbm, grad, res_out,
+    rows_ref, tables, res_buf, shift, staged, load_sem, small_sem, sem,
+):
     size = rows_ref.shape[1]
-    loads = [pltpu.make_async_copy(tables_hbm, tables, load_sem.at[0])]
-    for t in range(PIECES):
-        loads.append(pltpu.make_async_copy(rows_hbm.at[pl.ds(t * size, size)], rows_ref.at[t], load_sem.at[t + 1]))
-    last = pltpu.make_async_copy(res_in, res_buf, load_sem.at[PIECES + 1])
-    for load in loads + [last]:
+    words = pltpu.make_async_copy(shift_hbm, shift, small_sem.at[1])
+    load_tables = pltpu.make_async_copy(tables_hbm, tables, small_sem.at[0])
+    loads = [
+        pltpu.make_async_copy(rows_hbm.at[pl.ds(t * size, size)], rows_ref.at[t], load_sem.at[t]) for t in range(PIECES)
+    ]
+    last = pltpu.make_async_copy(res_in, res_buf, small_sem.at[2])
+    for load in [load_tables, loads[0], words] + loads[1:] + [last]:
         load.start()
-    loads[0].wait()
+    load_tables.wait()
     stores = []
     for t in range(PIECES):
-        loads[t + 1].wait()
-        for layer in range(LOCAL):
-            span = slice(layer * BLOCK, (layer + 1) * BLOCK)
-            pieces = banded(lambda low: rows_ref[t, :, low : low + BLOCK], tables[0, span], tables[1, span])
-            for q, piece in enumerate(pieces):
-                staged[t, layer, :, q * HALF : (q + 1) * HALF] = piece.astype(jnp.bfloat16)
-            store = pltpu.make_async_copy(
-                staged.at[t, layer], grad.at[layer, pl.ds(t * size, size)], sem.at[t * LOCAL + layer]
-            )
-            store.start()
-            stores.append(store)
+        loads[t].wait()
+        empty = jnp.zeros((size, HALF), jnp.bfloat16)
+        windows = [jnp.concatenate([empty, rows_ref[t, :, :HALF]], axis=1)]
+        windows += [rows_ref[t, :, q * HALF : q * HALF + BLOCK] for q in range(3)]
+        windows += [jnp.concatenate([rows_ref[t, :, 3 * HALF :], empty], axis=1)]
+        if t == 0:
+            words.wait()
+        for pair in range(LOCAL // 2):
+            for n, window in enumerate(windows):
+                wide = jnp.dot(window, tables[pair], preferred_element_type=jnp.float32).astype(jnp.bfloat16)
+                for half in range(2):
+                    staged[t, 2 * pair + half, :, n * HALF : (n + 1) * HALF] = wide[:, half * HALF : (half + 1) * HALF]
+            for layer in (2 * pair, 2 * pair + 1):
+                first = pl.multiple_of(jnp.where(shift[layer] < 0, 0, HALF), HALF)
+                store = pltpu.make_async_copy(
+                    staged.at[t, layer, :, pl.ds(first, X)],
+                    grad.at[layer, pl.ds(t * size, size)],
+                    sem.at[t * LOCAL + layer],
+                )
+                store.start()
+                stores.append(store)
         if t == 0:
             last.wait()
-            keep = pltpu.make_async_copy(res_buf, res_out, load_sem.at[0])
+            keep = pltpu.make_async_copy(res_buf, res_out, small_sem.at[0])
             keep.start()
             stores.append(keep)
     for store in stores:
@@ -294,7 +328,7 @@
         exchange,
         out_shape=(
             jax.ShapeDtypeStruct((8, 2, 8, 2, coefs, cols), jnp.bfloat16),
-            jax.ShapeDtypeStruct((2, tall, BLOCK), jnp.bfloat16),
+            jax.ShapeDtypeStruct((layers // 2, BLOCK, BLOCK), jnp.bfloat16),
             jax.ShapeDtypeStruct(data.shape, jnp.bfloat16),
         ),
         in_specs=[hbm] * 6,
@@ -305,8 +339,7 @@
             pltpu.SMEM(frac.shape, jnp.int32),
             pltpu.VMEM((tall, BLOCK), jnp.bfloat16),
             pltpu.VMEM((tall, BLOCK), jnp.bfloat16),
-            pltpu.VMEM((tall, BLOCK), jnp.bfloat16),
-            pltpu.VMEM((tall, BLOCK), jnp.bfloat16),
+            pltpu.VMEM((layers // 2, BLOCK, BLOCK), jnp.bfloat16),
             pltpu.VMEM((8, 8, 2, coefs, cols), jnp.bfloat16),
             pltpu.VMEM(data.shape, jnp.bfloat16),
             pltpu.VMEM((8, 2, 8, 2, coefs, cols), jnp.float32),
@@ -330,19 +363,21 @@
             jax.ShapeDtypeStruct((layers, flat, cols), jnp.bfloat16),
             jax.ShapeDtypeStruct(data.shape, jnp.bfloat16),
         ),
-        in_specs=[hbm] * 3,
+        in_specs=[hbm] * 4,
         out_specs=(hbm, hbm),
         scratch_shapes=[
             pltpu.VMEM((PIECES, flat // PIECES, cols), jnp.bfloat16),
-            pltpu.VMEM((2, tall, BLOCK), jnp.bfloat16),
+            pltpu.VMEM((layers // 2, BLOCK, BLOCK), jnp.bfloat16),
             pltpu.VMEM(data.shape, jnp.bfloat16),
-            pltpu.VMEM((PIECES, layers, flat // PIECES, cols), jnp.bfloat16),
-            dma((PIECES + 2,)),
+            pltpu.SMEM(shift.shape, jnp.int32),
+            pltpu.VMEM((PIECES, layers, flat // PIECES, cols + HALF), jnp.bfloat16),
+            dma((PIECES,)),
+            dma((3,)),
             dma((PIECES * layers,)),
         ],
         compiler_params=pltpu.CompilerParams(vmem_limit_bytes=VMEM),
         name="back_project",
-    )(grad_rows.reshape(flat, cols), tables, resid)
+    )(grad_rows.reshape(flat, cols), tables, resid, shift)
     return gradient.reshape(volume.shape), residual
 
 

time: 49.3 us -> 48.3 us (0.980)
  Pallas kernels: 48.5 us -> 47.5 us
    pallas_call x1, Pallas kernels: 42.1 us -> 41.5 us  [shards(): pl.pallas_call(exchange, out_shape=(jax.ShapeDtypeStruct((8, 2, 8, 2, coe...]
where the time goes in v3:
time: 48.3 us; the launch traced here: 48.2 us
  Pallas kernels  47.5 us (98%)
  between operations  0.64 us (1%)
    pallas_call x1, Pallas kernels, shards(): pl.pallas_call(exchange, out_shape=(jax.ShapeDtypeStruct((8, 2, 8, 2, coe...  41.5 us
    pallas_call x1, Pallas kernels, shards(): pl.pallas_call(back_project, out_shape=(jax.ShapeDtypeStruct((layers, fla...  6 us

profile of v3, /device:TPU:1, one launch (start us, length us, event | category | flops | bytes accessed | tf_op | source)
XLA Modules:
  0.0 48.2 jit_solution(12595209228345630923)
XLA Ops:
  0.6 41.5 %exchange.1 = (bf16[8,2,8,2,8,512]{5,4,3,2,1,0:T(8,128)(2,1)}, bf16[2,256,256]{2,1,0:T(8,128)(2,1)}, bf16[2,64,512]{2,1,0:T(8,128)(2,1)}) custom-call(bf16[4,2048,512]{2,1,0:T(8,128)(2,1)} %bitcast.3, s32[4]{0:T(128)} %shift_hbm.3, s32[4]{0:T(128)} %frac_hbm.1, bf16[64,64]{1,0:T(8,128)(2,1)} %basis.1, f32[2,64,512]{2,1,0:T(8,128)} %data.1, s32[2,64,512]{2,1,0:T(8,128)} %mask.1), custom_call_target="tpu_custom_call" | custom-call | tf_op jit(solution)/shard_map/exchange/pallas_call | solution.py:327
  42.2 6.0 %back_project.1 = (bf16[4,2048,512]{2,1,0:T(8,128)(2,1)}, bf16[2,64,512]{2,1,0:T(8,128)(2,1)}) custom-call(bf16[2048,512]{1,0:T(8,128)(2,1)} %bitcast.4, bf16[2,256,256]{2,1,0:T(8,128)(2,1)} %get-tuple-element.8.tables_hbm, bf16[2,64,512]{2,1,0:T(8,128)(2,1)} %get-tuple-element.9.res_in, s32[4]{0:T(128)} %shift_hbm.3), custom_call_target="tpu_custom_call" | custom-call | tf_op jit(solution)/shard_map/back_project/pallas_call | solution.py:360

commit v4 on v3

--- a/solution.py
+++ b/solution.py
@@ -19,7 +19,7 @@
 )[:0:-1]
 GROUPS = ((0, 4), (4, 2), (6, 2))
 VMEM = 60 * 1024 * 1024
-PIECES = 4
+PIECES = ((0, 512), (512, 1024), (1536, 512))
 ORDER = ((1, 0), (0, 1), (2, 0), (3, 1), (1, 1), (2, 1), (3, 0), (0, 0))
 KEPT = tuple(7 if pair == (0, 0) else 8 for pair in ORDER)
 
@@ -276,35 +276,36 @@
     rows_hbm, tables_hbm, res_in, shift_hbm, grad, res_out,
     rows_ref, tables, res_buf, shift, staged, load_sem, small_sem, sem,
 ):
-    size = rows_ref.shape[1]
     words = pltpu.make_async_copy(shift_hbm, shift, small_sem.at[1])
     load_tables = pltpu.make_async_copy(tables_hbm, tables, small_sem.at[0])
     loads = [
-        pltpu.make_async_copy(rows_hbm.at[pl.ds(t * size, size)], rows_ref.at[t], load_sem.at[t]) for t in range(PIECES)
+        pltpu.make_async_copy(rows_hbm.at[pl.ds(low, size)], rows_ref.at[pl.ds(low, size)], load_sem.at[t])
+        for t, (low, size) in enumerate(PIECES)
     ]
     last = pltpu.make_async_copy(res_in, res_buf, small_sem.at[2])
     for load in [load_tables, loads[0], words] + loads[1:] + [last]:
         load.start()
     load_tables.wait()
     stores = []
-    for t in range(PIECES):
+    for t, (low, size) in enumerate(PIECES):
+        span = pl.ds(low, size)
         loads[t].wait()
         empty = jnp.zeros((size, HALF), jnp.bfloat16)
-        windows = [jnp.concatenate([empty, rows_ref[t, :, :HALF]], axis=1)]
-        windows += [rows_ref[t, :, q * HALF : q * HALF + BLOCK] for q in range(3)]
-        windows += [jnp.concatenate([rows_ref[t, :, 3 * HALF :], empty], axis=1)]
+        windows = [jnp.concatenate([empty, rows_ref[span, :HALF]], axis=1)]
+        windows += [rows_ref[span, q * HALF : q * HALF + BLOCK] for q in range(3)]
+        windows += [jnp.concatenate([rows_ref[span, 3 * HALF :], empty], axis=1)]
         if t == 0:
             words.wait()
         for pair in range(LOCAL // 2):
             for n, window in enumerate(windows):
                 wide = jnp.dot(window, tables[pair], preferred_element_type=jnp.float32).astype(jnp.bfloat16)
                 for half in range(2):
-                    staged[t, 2 * pair + half, :, n * HALF : (n + 1) * HALF] = wide[:, half * HALF : (half + 1) * HALF]
+                    staged[2 * pair + half, span, n * HALF : (n + 1) * HALF] = wide[:, half * HALF : (half + 1) * HALF]
             for layer in (2 * pair, 2 * pair + 1):
                 first = pl.multiple_of(jnp.where(shift[layer] < 0, 0, HALF), HALF)
                 store = pltpu.make_async_copy(
-                    staged.at[t, layer, :, pl.ds(first, X)],
-                    grad.at[layer, pl.ds(t * size, size)],
+                    staged.at[layer, span, pl.ds(first, X)],
+                    grad.at[layer, span],
                     sem.at[t * LOCAL + layer],
                 )
                 store.start()
@@ -366,14 +367,14 @@
         in_specs=[hbm] * 4,
         out_specs=(hbm, hbm),
         scratch_shapes=[
-            pltpu.VMEM((PIECES, flat // PIECES, cols), jnp.bfloat16),
+            pltpu.VMEM((flat, cols), jnp.bfloat16),
             pltpu.VMEM((layers // 2, BLOCK, BLOCK), jnp.bfloat16),
             pltpu.VMEM(data.shape, jnp.bfloat16),
             pltpu.SMEM(shift.shape, jnp.int32),
-            pltpu.VMEM((PIECES, layers, flat // PIECES, cols + HALF), jnp.bfloat16),
-            dma((PIECES,)),
+            pltpu.VMEM((layers, flat, cols + HALF), jnp.bfloat16),
+            dma((len(PIECES),)),
             dma((3,)),
-            dma((PIECES * layers,)),
+            dma((len(PIECES) * layers,)),
         ],
         compiler_params=pltpu.CompilerParams(vmem_limit_bytes=VMEM),
         name="back_project",

time: 48.3 us -> 48.1 us (level)
  no operation moved by 1% of the time
where the time goes in v4:
time: 48.1 us; the launch traced here: 48 us
  Pallas kernels  47.4 us (99%)
  between operations  0.64 us (1%)
    pallas_call x1, Pallas kernels, shards(): pl.pallas_call(exchange, out_shape=(jax.ShapeDtypeStruct((8, 2, 8, 2, coe...  41.5 us
    pallas_call x1, Pallas kernels, shards(): pl.pallas_call(back_project, out_shape=(jax.ShapeDtypeStruct((layers, fla...  5.85 us

profile of v4, /device:TPU:1, one launch (start us, length us, event | category | flops | bytes accessed | tf_op | source)
XLA Modules:
  0.0 48.0 jit_solution(18113084091328557864)
XLA Ops:
  0.6 41.5 %exchange.1 = (bf16[8,2,8,2,8,512]{5,4,3,2,1,0:T(8,128)(2,1)}, bf16[2,256,256]{2,1,0:T(8,128)(2,1)}, bf16[2,64,512]{2,1,0:T(8,128)(2,1)}) custom-call(bf16[4,2048,512]{2,1,0:T(8,128)(2,1)} %bitcast.3, s32[4]{0:T(128)} %shift_hbm.3, s32[4]{0:T(128)} %frac_hbm.1, bf16[64,64]{1,0:T(8,128)(2,1)} %basis.1, f32[2,64,512]{2,1,0:T(8,128)} %data.1, s32[2,64,512]{2,1,0:T(8,128)} %mask.1), custom_call_target="tpu_custom_call" | custom-call | tf_op jit(solution)/shard_map/exchange/pallas_call | solution.py:328
  42.2 5.9 %back_project.1 = (bf16[4,2048,512]{2,1,0:T(8,128)(2,1)}, bf16[2,64,512]{2,1,0:T(8,128)(2,1)}) custom-call(bf16[2048,512]{1,0:T(8,128)(2,1)} %bitcast.4, bf16[2,256,256]{2,1,0:T(8,128)(2,1)} %get-tuple-element.8.tables_hbm, bf16[2,64,512]{2,1,0:T(8,128)(2,1)} %get-tuple-element.9.res_in, s32[4]{0:T(128)} %shift_hbm.3), custom_call_target="tpu_custom_call" | custom-call | tf_op jit(solution)/shard_map/back_project/pallas_call | solution.py:361

commit v5 on v4

--- a/solution.py
+++ b/solution.py
@@ -19,7 +19,7 @@
 )[:0:-1]
 GROUPS = ((0, 4), (4, 2), (6, 2))
 VMEM = 60 * 1024 * 1024
-PIECES = ((0, 512), (512, 1024), (1536, 512))
+PIECES = ((0, 512), (512, 1280), (1792, 256))
 ORDER = ((1, 0), (0, 1), (2, 0), (3, 1), (1, 1), (2, 1), (3, 0), (0, 0))
 KEPT = tuple(7 if pair == (0, 0) else 8 for pair in ORDER)
 

time: 48.1 us -> 48.4 us (level)
  no operation moved by 1% of the time
where the time goes in v5:
time: 48.4 us; the launch traced here: 48.3 us
  Pallas kernels  47.7 us (99%)
  between operations  0.64 us (1%)
    pallas_call x1, Pallas kernels, shards(): pl.pallas_call(exchange, out_shape=(jax.ShapeDtypeStruct((8, 2, 8, 2, coe...  41.5 us
    pallas_call x1, Pallas kernels, shards(): pl.pallas_call(back_project, out_shape=(jax.ShapeDtypeStruct((layers, fla...  6.14 us

profile of v5, /device:TPU:1, one launch (start us, length us, event | category | flops | bytes accessed | tf_op | source)
XLA Modules:
  0.0 48.3 jit_solution(14964075815184243377)
XLA Ops:
  0.6 41.5 %exchange.1 = (bf16[8,2,8,2,8,512]{5,4,3,2,1,0:T(8,128)(2,1)}, bf16[2,256,256]{2,1,0:T(8,128)(2,1)}, bf16[2,64,512]{2,1,0:T(8,128)(2,1)}) custom-call(bf16[4,2048,512]{2,1,0:T(8,128)(2,1)} %bitcast.3, s32[4]{0:T(128)} %shift_hbm.3, s32[4]{0:T(128)} %frac_hbm.1, bf16[64,64]{1,0:T(8,128)(2,1)} %basis.1, f32[2,64,512]{2,1,0:T(8,128)} %data.1, s32[2,64,512]{2,1,0:T(8,128)} %mask.1), custom_call_target="tpu_custom_call" | custom-call | tf_op jit(solution)/shard_map/exchange/pallas_call | solution.py:328
  42.2 6.1 %back_project.1 = (bf16[4,2048,512]{2,1,0:T(8,128)(2,1)}, bf16[2,64,512]{2,1,0:T(8,128)(2,1)}) custom-call(bf16[2048,512]{1,0:T(8,128)(2,1)} %bitcast.4, bf16[2,256,256]{2,1,0:T(8,128)(2,1)} %get-tuple-element.8.tables_hbm, bf16[2,64,512]{2,1,0:T(8,128)(2,1)} %get-tuple-element.9.res_in, s32[4]{0:T(128)} %shift_hbm.3), custom_call_target="tpu_custom_call" | custom-call | tf_op jit(solution)/shard_map/back_project/pallas_call | solution.py:361
